TPU v7x, 256 devices: a whole 4x4x8 slice. The times are simulated.
256 devices in a mesh: dp: 16 (over x, z_lo), hyper: 16 (over y, z_hi, core).
Axes of the slice: x: 4, y: 4, z: 8 (z_hi: 2, z_lo: 4; z = z_hi * 4 + z_lo), core: 2. Of those that a mesh axis runs over, the one named last changes fastest.
Arguments:
- inputs: bfloat16 [512, 64, 128], P(('dp', 'hyper')), may hold values from -64 to 64
- labels: int32 [512, 64], P(('dp', 'hyper')), may hold values from 0 to 255
- client_ids: int32 [512], P(('dp', 'hyper')), may hold values from 0 to 511
- ext_weight: bfloat16 [128, 4096], replicated, may hold values from -0.5 to 0.5
- ext_bias: bfloat16 [4096], replicated, may hold values from -3 to 3
- embeddings: bfloat16 [512, 128], replicated, may hold values from -1.5 to 1.5
- hyper_in: bfloat16 [128, 50], replicated, may hold values from -2.09375 to 2.09375
- hyper_bias: float32 [50], replicated, may hold values from -3 to 3
- hyper_out: bfloat16 [4096, 50, 256], P('hyper'), may hold values from -0.1796875 to 0.1796875
Outputs:
- grad_ext_weight: float32 [128, 4096], replicated
- grad_ext_bias: float32 [4096], replicated
- grad_embeddings: float32 [512, 128], replicated
- grad_hyper_in: float32 [128, 50], replicated
- grad_hyper_bias: float32 [50], replicated
- grad_hyper_out: float32 [4096, 50, 256], P(('hyper', 'dp'))
Inputs may be any that keep to these rules, and one draw needn't show every extreme that they name: `client_ids`: A client may hold several slots or none.
All inputs are finite; a program needn't handle non-finite values.
Results may differ from a plain program's by a relative error of at most 0.014.
The roundings to bfloat16 on the way count: a program that leaves them out, or rounds other values in their place, can miss the bound.
Values may be sent and summed in bfloat16 or wider, within the bound.
No kernel may reach another device: no remote copies, remote signals or barrier semaphores. Data moves between devices by JAX's collectives and lax.ppermute only.
A program may use at most 128 MiB of HBM per device.

v0:
```python
import jax
import jax.numpy as jnp
from jax import lax
from jax.sharding import Mesh
from jax.sharding import PartitionSpec as P

DP = ("dp_0", "dp_1")
DP_HYPER = ("dp_0", "dp_1", "hyper")
HYPER_DP = ("hyper", "dp_0", "dp_1")


def sent_to_all(value, axis):
    copies = jnp.broadcast_to(value, (lax.axis_size(axis), *value.shape))
    return lax.all_to_all(copies, axis, split_axis=0, concat_axis=0, tiled=True)


def laid_out(tiles, dim):
    lengths = list(tiles.shape[1:])
    lengths[dim] *= tiles.shape[0]
    return jnp.moveaxis(tiles, 0, dim).reshape(lengths)


def gather_directly(value, axis, dim):
    tiles = sent_to_all(value, axis)
    return laid_out(tiles, dim)


def own_rows(terms, axes):
    total = terms.astype(jnp.bfloat16)
    for axis in axes:
        total = lax.psum_scatter(total, axis, scatter_dimension=0, tiled=True)
    return total.astype(jnp.float32)


def silu_slope(values):
    logistic = jax.nn.sigmoid(values)
    return logistic * (1.0 + values * (1.0 - logistic))


def class_grads(logits, slot_labels, row_count):
    largest = jnp.max(logits, axis=-1, keepdims=True)
    exponent = jnp.exp(logits - largest)
    probability = exponent / jnp.sum(exponent, axis=-1, keepdims=True)
    classes = jnp.arange(logits.shape[-1], dtype=jnp.int32)
    onehot = (slot_labels[..., None] == classes).astype(jnp.float32)
    return ((probability - onehot) / row_count).astype(jnp.bfloat16)


def local(
    inputs, labels, client_ids, ext_weight, ext_bias, embeddings, hyper_in, hyper_bias, hyper_out
):
    slot_count, row_count, width_in = inputs.shape
    width = ext_weight.shape[1]
    flat_in = inputs.reshape(slot_count * row_count, width_in)
    preact = jnp.dot(flat_in, ext_weight, preferred_element_type=jnp.float32) + ext_bias.astype(
        jnp.float32
    )
    features = jax.nn.silu(preact).astype(jnp.bfloat16).reshape(slot_count, row_count, width)
    row_ids = gather_directly(client_ids, "hyper", 0)
    table_ids = jnp.arange(embeddings.shape[0], dtype=jnp.int32)
    select = (row_ids[:, None] == table_ids[None, :]).astype(jnp.bfloat16)
    picked = jnp.dot(select, embeddings, preferred_element_type=jnp.float32).astype(jnp.bfloat16)
    hyper_preact = jnp.dot(picked, hyper_in, preferred_element_type=jnp.float32) + hyper_bias
    hidden = jax.nn.silu(hyper_preact).astype(jnp.bfloat16)
    head_part = jnp.einsum(
        "kh,dhc->kdc", hidden, hyper_out, preferred_element_type=jnp.float32
    ).astype(jnp.bfloat16)
    feat_cols = lax.all_to_all(features, "hyper", split_axis=2, concat_axis=0, tiled=True)
    logits = lax.psum_scatter(
        jnp.einsum("krd,kdc->krc", feat_cols, head_part, preferred_element_type=jnp.float32),
        "hyper",
        scatter_dimension=0,
        tiled=True,
    )
    dlogits = class_grads(logits, labels, row_count)
    dlog_rows = lax.all_gather(dlogits, "hyper", axis=0, tiled=True)
    dhead_part = jnp.einsum(
        "krd,krc->kdc", feat_cols, dlog_rows, preferred_element_type=jnp.float32
    ).astype(jnp.bfloat16)
    dfeat_cols = jnp.einsum(
        "krc,kdc->krd", dlog_rows, head_part, preferred_element_type=jnp.float32
    ).astype(jnp.bfloat16)
    dfeatures = lax.all_to_all(dfeat_cols, "hyper", split_axis=0, concat_axis=2, tiled=True)
    dpreact = (
        dfeatures.reshape(slot_count * row_count, width).astype(jnp.float32) * silu_slope(preact)
    ).astype(jnp.bfloat16)
    grad_weight = jnp.dot(flat_in.T, dpreact, preferred_element_type=jnp.float32)
    grad_bias = jnp.sum(dpreact.astype(jnp.float32), axis=0)
    grad_out = own_rows(
        jnp.einsum("kh,kdc->dhc", hidden, dhead_part, preferred_element_type=jnp.float32), DP
    )
    dhidden = jnp.einsum("kdc,dhc->kh", dhead_part, hyper_out, preferred_element_type=jnp.float32)
    hyper_dpre = dhidden * silu_slope(hyper_preact)
    grad_in = jnp.dot(picked.astype(jnp.float32).T, hyper_dpre)
    grad_hbias = jnp.sum(hyper_dpre, axis=0)
    back_rows = jnp.dot(hyper_dpre, hyper_in.astype(jnp.float32).T)
    grad_table = jnp.dot(select.astype(jnp.float32).T, back_rows)
    grad_weight, grad_bias, grad_table, grad_in, grad_hbias = lax.psum(
        (grad_weight, grad_bias, grad_table, grad_in, grad_hbias), DP_HYPER
    )
    return (grad_weight, grad_bias, grad_table, grad_in, grad_hbias, grad_out)


def solution(mesh):
    torus = Mesh(mesh.devices.reshape(4, 4, mesh.shape["hyper"]), ("dp_0", "dp_1", "hyper"))
    placed = (
        P(DP_HYPER, None, None),
        P(DP_HYPER, None),
        P(DP_HYPER),
        P(),
        P(),
        P(),
        P(),
        P(),
        P("hyper", None, None),
    )
    return jax.shard_map(
        local,
        mesh=torus,
        in_specs=placed,
        out_specs=(P(), P(), P(), P(), P(), P(HYPER_DP, None, None)),
        check_vma=False,
    )
```

profile of v0, /device:TPU:1, one launch (start us, length us, event | category | flops | bytes accessed | tf_op | source)
XLA Modules:
  0.0 629.8 jit_solution(14461696702569586145)
XLA Ops:
  7.2 0.0 copy-start
  7.2 1.3 broadcast_in_dim.2
  8.5 12.6 %all-to-all-start.1 = ((s32[16,1,2]{2,1,0:T(1,128)}), s32[16,1,2]{2,1,0:T(1,128)S(1)}, u32[]{:S(2)}, u32[]{:S(2)}) async-start(s32[16,1,2]{2,1,0:T(1,128)} %broadcast_in_dim.2), calls=%async_computation.1 | async-start | bytes 16384 | tf_op jit(solution)/shard_map/all_to_all | solution.py:14
  21.1 0.7 convert_element_type.58
  21.8 0.0 copy-done
  21.8 3.1 multiply_convert_fusion.1
  24.9 5.0 copy.35
  30.0 0.0 copy-start.8
  30.0 0.0 copy-start.5
  30.0 0.0 copy-start.7
  30.0 2.2 reshape.50
  32.3 0.0 all-to-all-done.1
  32.3 9.6 %all-to-all-start = ((bf16[16,2,16384]{2,1,0:T(2,128)(2,1)}), bf16[16,2,16384]{2,1,0:T(2,128)(2,1)S(1)}, u32[]{:S(2)}, u32[]{:S(2)}) async-start(bf16[16,2,16384]{2,1,0:T(2,128)(2,1)} %reshape.50), calls=%async_computation | async-start | bytes 2097152 | tf_op jit(solution)/shard_map/all_to_all | solution.py:68
  41.9 0.0 reduce-scatter.4.cloned.1.call-start
  41.9 0.5 broadcast.18
  42.4 0.7 reduce.3
  43.1 0.1 eq.28
  43.2 0.0 copy-done.8
  43.2 0.2 convolution_convert_fusion.1
  43.4 0.1 convolution_add_fusion.1
  43.6 10.5 %fusion.9 = bf16[32,256,256]{2,0,1:T(8,128)(2,1)} fusion(bf16[256,50,256]{2,0,1:T(8,128)(2,1)} %param.17, f32[32,50]{1,0:T(8,128)S(1)} %convolution_add_fusion.1), kind=kOutput, calls=%fused_computation.12 | convolution fusion | flops 211820352 | bytes 10754304 | tf_op jit(solution)/shard_map/kh,dhc->kdc/dot_general | solution.py:65
  54.1 9.6 %all-to-all-done = bf16[16,2,16384]{2,1,0:T(2,128)(2,1)S(1)} async-done(((bf16[16,2,16384]{2,1,0:T(2,128)(2,1)}), bf16[16,2,16384]{2,1,0:T(2,128)(2,1)S(1)}, u32[]{:S(2)}, u32[]{:S(2)}) %all-to-all-start) | async-done | bytes 1048608 | tf_op jit(solution)/shard_map/all_to_all | solution.py:68
  63.7 2.4 reshape.51
  66.1 4.5 copy.36
  70.6 6.0 fusion.7
  76.5 0.0 reduce-scatter.4.cloned.1.call-update
  76.6 0.0 all-gather.2.cloned.1.call-start
  76.6 89.9 %reduce-scatter.4.cloned.1.call-done = f32[2,64,256]{2,1,0:T(8,128)} async-done(((f32[32,64,256]{2,1,0:T(8,128)}), f32[2,64,256]{2,1,0:T(8,128)}) %reduce-scatter.4.cloned.1.call-update) | async-done | bytes 131088 | tf_op jit(solution)/shard_map/reduce_scatter | solution.py:69
  166.5 1.9 fusion.20
  168.4 0.0 all-gather.2.cloned.1.call-update
  168.4 0.2 reduce-scatter.6.cloned.1.call-start
  168.7 55.2 %all-gather.2.cloned.1.call-done = bf16[32,64,256]{2,1,0:T(8,128)(2,1)} async-done(((bf16[2,64,256]{2,1,0:T(8,128)(2,1)}), bf16[32,64,256]{2,1,0:T(8,128)(2,1)}) %all-gather.2.cloned.1.call-update) | async-done | bytes 1048592 | tf_op jit(solution)/shard_map/all_gather | solution.py:76
  223.8 2.5 convolution_convert_fusion
  226.4 0.0 copy-start.1
  226.4 2.0 copy-done.1
  228.3 6.0 convert_bitcast_fusion
  234.4 0.0 reduce-scatter.6.cloned.1.call-update
  234.4 1.2 copy-done.2
  235.6 5.7 fusion.12
  241.3 4.0 all-to-all-start.2
  245.3 0.3 all-reduce.4.cloned.1.call-start
  245.6 11.3 %copy.42 = bf16[256,50,256]{0,1,2:T(8,128)(2,1)} copy(bf16[256,50,256]{2,0,1:T(8,128)(2,1)} %param.17) | data formatting | bytes 13107200 | tf_op args[8]
  256.9 8.0 %copy.41 = bf16[32,256,256]{1,0,2:T(8,128)(2,1)} copy(bf16[32,256,256]{2,1,0:T(8,128)(2,1)} %copy-done.1) | data formatting | bytes 8388608 | tf_op jit(solution)/shard_map/convert_element_type | solution.py:79
  264.9 6.5 %fusion.30 = (f32[50]{0:T(128)S(1)}, bf16[32,50]{1,0:T(8,128)(2,1)S(1)}) fusion(f32[32,50]{1,0:T(8,128)S(1)} %convolution_add_fusion.1, bf16[32,256,256]{1,0,2:T(8,128)(2,1)} %copy.41, bf16[256,50,256]{0,1,2:T(8,128)(2,1)} %copy.42), kind=kOutput, calls=%fused_computation.40 | convolution fusion | flops 209731152 | bytes 10757704 | tf_op jit(solution)/shard_map/kdc,dhc->kh/dot_general | solution.py:92
  271.4 1.0 fusion.21
  272.4 0.0 all-to-all-done.2
  272.4 0.6 copy.40
  273.0 0.0 copy-start.3
  273.1 1.7 copy.46
  274.7 0.0 copy-start.6
  274.7 0.8 convert_reduce_fusion
  275.6 0.0 copy-done.6
  275.6 1.8 convolution_bitcast_fusion
  277.4 0.0 all-reduce.4.cloned.1.call-update
  277.4 0.0 reduce-scatter.8.cloned.1.call-start
  277.5 27.3 %reduce-scatter.6.cloned.1.call-done = bf16[64,50,256]{2,1,0:T(8,128)(2,1)} async-done(((bf16[256,50,256]{2,1,0:T(8,128)(2,1)}), bf16[64,50,256]{2,1,0:T(8,128)(2,1)}) %reduce-scatter.6.cloned.1.call-update) | async-done | bytes 1638416 | tf_op jit(solution)/shard_map/reduce_scatter | solution.py:31
  304.8 0.0 reduce-scatter.8.cloned.1.call-update
  304.8 0.2 fusion.31
  305.0 76.7 %all-reduce = (f32[4096]{0:T(1024)}, f32[128,50]{0,1:T(8,128)}, f32[50]{0:T(128)}) all-reduce(f32[4096]{0:T(1024)S(1)} %get-tuple-element.29, f32[128,50]{0,1:T(8,128)S(1)} %fusion.31, f32[50]{0:T(128)S(1)} %get-tuple-element.33), channel_id=1, replica_groups=mesh['dp_0'=4,'dp_1'=4,'hyper'=16] {'dp_0','dp_1','hyper'}, use_global_device_ids=true, to_apply=%region_5.6 | all-reduce | flops 10546 | bytes 84368 | tf_op jit(solution)/shard_map/psum | solution.py:98
  381.7 191.7 %all-reduce.4.cloned.1.call-done = (f32[128,4096]{0,1:T(8,128)}, f32[512,128]{1,0:T(8,128)}) async-done(((f32[128,4096]{0,1:T(8,128)}, f32[512,128]{1,0:T(8,128)}), (f32[128,4096]{0,1:T(8,128)}, f32[512,128]{1,0:T(8,128)})) %all-reduce.4.cloned.1.call-update) | async-done | bytes 2359312 | tf_op jit(solution)/shard_map/psum | solution.py:98
  573.3 2.9 copy.44
  576.3 44.3 %reduce-scatter.8.cloned.1.call-done = bf16[16,50,256]{2,1,0:T(8,128)(2,1)} async-done(((bf16[64,50,256]{2,1,0:T(8,128)(2,1)}), bf16[16,50,256]{2,1,0:T(8,128)(2,1)}) %reduce-scatter.8.cloned.1.call-update) | async-done | bytes 409616 | tf_op jit(solution)/shard_map/reduce_scatter | solution.py:31
  620.6 2.0 copy.45
  622.6 0.7 copy.61
  (8 shorter events, 0.0 us)
Async XLA Ops:
  7.2 14.7 %copy-start = (bf16[128,4096]{1,0:T(8,128)(2,1)S(1)}, bf16[128,4096]{1,0:T(8,128)(2,1)}, u32[]{:S(2)}) copy-start(bf16[128,4096]{1,0:T(8,128)(2,1)} %param.12) | copy-start | bytes 3145732
  8.5 23.7 %all-to-all-start.1 = ((s32[16,1,2]{2,1,0:T(1,128)}), s32[16,1,2]{2,1,0:T(1,128)S(1)}, u32[]{:S(2)}, u32[]{:S(2)}) async-start(s32[16,1,2]{2,1,0:T(1,128)} %broadcast_in_dim.2), calls=%async_computation.1 | async-start | bytes 16384 | tf_op jit(solution)/shard_map/all_to_all | solution.py:14
  30.0 13.2 %copy-start.8 = (bf16[512,128]{1,0:T(8,128)(2,1)S(1)}, bf16[512,128]{1,0:T(8,128)(2,1)}, u32[]{:S(2)}) copy-start(bf16[512,128]{1,0:T(8,128)(2,1)} %param.14) | copy-start | bytes 393220
  30.0 13.4 %copy-start.5 = (bf16[128,50]{0,1:T(8,128)(2,1)S(1)}, bf16[128,50]{0,1:T(8,128)(2,1)}, u32[]{:S(2)}) copy-start(bf16[128,50]{0,1:T(8,128)(2,1)} %param.15) | copy-start | bytes 38404
  30.0 13.4 %copy-start.7 = (f32[50]{0:T(128)S(1)}, f32[50]{0:T(128)}, u32[]{:S(2)}) copy-start(f32[50]{0:T(128)} %param.16) | copy-start | bytes 604
  32.3 31.4 %all-to-all-start = ((bf16[16,2,16384]{2,1,0:T(2,128)(2,1)}), bf16[16,2,16384]{2,1,0:T(2,128)(2,1)S(1)}, u32[]{:S(2)}, u32[]{:S(2)}) async-start(bf16[16,2,16384]{2,1,0:T(2,128)(2,1)} %reshape.50), calls=%async_computation | async-start | bytes 2097152 | tf_op jit(solution)/shard_map/all_to_all | solution.py:68
  41.9 124.6 %reduce-scatter.4.cloned.1.call-start = ((), (), s32[]{:S(2)}) async-start(), calls=%async_computation.6 | async-start | bytes 2228224 | tf_op jit(solution)/shard_map/reduce_scatter | solution.py:69
  76.5 90.0 %copy-start.9 = (s32[2,64]{1,0:T(2,128)S(1)}, s32[2,64]{1,0:T(2,128)}, u32[]{:S(2)}) copy-start(s32[2,64]{1,0:T(2,128)} %param.10) | copy-start | bytes 1540
  76.6 147.3 %all-gather.2.cloned.1.call-start = ((), (), s32[]{:S(2)}) async-start(), calls=%async_computation.7 | async-start | bytes 1114112 | tf_op jit(solution)/shard_map/all_gather | solution.py:76
  168.4 136.4 %reduce-scatter.6.cloned.1.call-start = ((), (), s32[]{:S(2)}) async-start(), calls=%async_computation.8 | async-start | bytes 9175040 | tf_op jit(solution)/shard_map/reduce_scatter | solution.py:31
  226.4 2.0 copy-start.1
  234.4 1.2 copy-start.2
  241.3 31.1 %all-to-all-start.2 = ((bf16[32,64,256]{2,1,0:T(8,128)(2,1)}), bf16[32,64,256]{2,1,0:T(8,128)(2,1)S(1)}, u32[]{:S(2)}, u32[]{:S(2)}) async-start(bf16[32,64,256]{2,1,0:T(8,128)(2,1)} %fusion.12), calls=%async_computation.3 | async-start | bytes 2097152 | tf_op jit(solution)/shard_map/all_to_all | solution.py:83
  245.3 328.0 %all-reduce.4.cloned.1.call-start = ((), (), s32[]{:S(2)}) async-start(), calls=%async_computation.10 | async-start | bytes 4718592 | tf_op jit(solution)/shard_map/psum | solution.py:98
  273.0 1.7 copy-start.3
  274.7 0.8 copy-start.6
  277.4 343.2 %reduce-scatter.8.cloned.1.call-start = ((), (), s32[]{:S(2)}) async-start(), calls=%async_computation.9 | async-start | bytes 2293760 | tf_op jit(solution)/shard_map/reduce_scatter | solution.py:31
  573.3 49.3 %copy-start.4 = (f32[512,128]{1,0:T(8,128)S(1)}, f32[512,128]{1,0:T(8,128)}, u32[]{:S(2)}) copy-start(f32[512,128]{1,0:T(8,128)} %get-tuple-element.39) | copy-start | bytes 786436
Sparse Core Ops, SparseCore 0:
  76.7 89.7 reduce-scatter.3
  169.8 54.0 all-gather.1
  234.5 70.2 reduce-scatter.5
  310.7 262.5 all-reduce.3
  575.7 44.7 reduce-scatter.7
where the time goes:
time: 631 us; the launch traced here: 630 us
  waiting for transfers between devices  418 us (66%)
  blocking collectives  76.7 us (12%)
  local copies, waits for them, and re-layouts  46.5 us (7%)
  matrix products  43.7 us (7%)
  starting transfers between devices  26.8 us (4%)
  between operations  13.9 us (2%)
    psum x1, waiting for transfers between devices, local(): lax.psum((grad_weight, grad_bias, grad_table, grad_in, grad_hbias), DP_HY...  192 us
    reduce_scatter x1, waiting for transfers between devices, local(): lax.psum_scatter(jnp.einsum('krd,kdc->krc', feat_cols, head_part, preferr...  89.9 us
    psum x1, blocking collectives, local(): lax.psum((grad_weight, grad_bias, grad_table, grad_in, grad_hbias), DP_HY...  76.7 us
    reduce_scatter x2, waiting for transfers between devices, own_rows(): total = lax.psum_scatter(total, axis, scatter_dimension=0, tiled=True)  71.6 us
    all_gather x1, waiting for transfers between devices, local(): dlog_rows = lax.all_gather(dlogits, 'hyper', axis=0, tiled=True)  55.2 us
    unnamed x27, local copies, waits for them, and re-layouts  26.5 us
  transfers between devices with their start and end apart: 8, of which 6 were waited for; matrix products, arithmetic and copies ran while one was open for 10% of the time, Pallas kernels for 0%

commit v1 on v0

--- a/solution.py
+++ b/solution.py
@@ -7,6 +7,14 @@
 DP = ("dp_0", "dp_1")
 DP_HYPER = ("dp_0", "dp_1", "hyper")
 HYPER_DP = ("hyper", "dp_0", "dp_1")
+
+
+def recast_blocks_in(mine_x):
+    peer_axis = "dp_0"
+    bus_axis = ("dp_1", "hyper")
+    for idx in (bus_axis, peer_axis):
+        mine_x = jax.lax.psum(mine_x, axis_name=idx)
+    return mine_x
 
 
 def sent_to_all(value, axis):
@@ -95,8 +103,8 @@
     grad_hbias = jnp.sum(hyper_dpre, axis=0)
     back_rows = jnp.dot(hyper_dpre, hyper_in.astype(jnp.float32).T)
     grad_table = jnp.dot(select.astype(jnp.float32).T, back_rows)
-    grad_weight, grad_bias, grad_table, grad_in, grad_hbias = lax.psum(
-        (grad_weight, grad_bias, grad_table, grad_in, grad_hbias), DP_HYPER
+    grad_weight, grad_bias, grad_table, grad_in, grad_hbias = recast_blocks_in(
+        (grad_weight, grad_bias, grad_table, grad_in, grad_hbias)
     )
     return (grad_weight, grad_bias, grad_table, grad_in, grad_hbias, grad_out)
 

time: 631 us -> 875 us (1.39)
  the two profiles are of different devices: /device:TPU:1 before, /device:TPU:32 now
where the time goes in v1:
time: 875 us; the launch traced here: 873 us
  waiting for transfers between devices  416 us (48%)
  blocking collectives  329 us (38%)
  matrix products  46.7 us (5%)
  local copies, waits for them, and re-layouts  39.1 us (4%)
  starting transfers between devices  24.8 us (3%)
  between operations  14.3 us (2%)
    psum x2, blocking collectives, recast_blocks_in(): mine_x = jax.lax.psum(mine_x, axis_name=idx)  329 us
    psum x2, waiting for transfers between devices, recast_blocks_in(): mine_x = jax.lax.psum(mine_x, axis_name=idx)  181 us
    reduce_scatter x1, waiting for transfers between devices, local(): lax.psum_scatter(jnp.einsum('krd,kdc->krc', feat_cols, head_part, preferr...  81.4 us
    reduce_scatter x2, waiting for transfers between devices, own_rows(): total = lax.psum_scatter(total, axis, scatter_dimension=0, tiled=True)  78.6 us
    all_gather x1, waiting for transfers between devices, local(): dlog_rows = lax.all_gather(dlogits, 'hyper', axis=0, tiled=True)  53.8 us
    unnamed x27, local copies, waits for them, and re-layouts  22.4 us
    all_to_all x1, waiting for transfers between devices, local(): lax.all_to_all(features, 'hyper', split_axis=2, concat_axis=0, tiled=True)  19.6 us
  transfers between devices with their start and end apart: 9, of which 6 were waited for; matrix products, arithmetic and copies ran while one was open for 7% of the time, Pallas kernels for 0%

profile of v1, /device:TPU:32, one launch (start us, length us, event | category | flops | bytes accessed | tf_op | source)
XLA Modules:
  0.0 873.5 jit_solution(16151420607507288877)
XLA Ops:
  7.2 0.0 copy-start
  7.2 1.3 broadcast_in_dim.2
  8.5 10.3 %all-to-all-start.1 = ((s32[16,1,2]{2,1,0:T(1,128)}), s32[16,1,2]{2,1,0:T(1,128)S(1)}, u32[]{:S(2)}, u32[]{:S(2)}) async-start(s32[16,1,2]{2,1,0:T(1,128)} %broadcast_in_dim.2), calls=%async_computation.1 | async-start | bytes 16384 | tf_op jit(solution)/shard_map/all_to_all | solution.py:22
  18.8 0.7 convert_element_type.58
  19.5 3.1 multiply_convert_fusion.1
  22.6 5.0 copy.35
  27.7 0.0 copy-start.8
  27.7 0.0 copy-start.5
  27.7 0.0 copy-start.7
  27.7 2.2 reshape.50
  30.0 0.0 all-to-all-done.1
  30.0 9.6 %all-to-all-start = ((bf16[16,2,16384]{2,1,0:T(2,128)(2,1)}), bf16[16,2,16384]{2,1,0:T(2,128)(2,1)S(1)}, u32[]{:S(2)}, u32[]{:S(2)}) async-start(bf16[16,2,16384]{2,1,0:T(2,128)(2,1)} %reshape.50), calls=%async_computation | async-start | bytes 2097152 | tf_op jit(solution)/shard_map/all_to_all | solution.py:76
  39.6 0.0 reduce-scatter.4.cloned.1.call-start
  39.6 0.5 broadcast.18
  40.2 0.7 reduce.3
  40.8 0.1 eq.28
  40.9 0.0 copy-done.8
  40.9 0.2 convolution_convert_fusion.1
  41.1 0.1 convolution_add_fusion.1
  41.3 10.4 %fusion.9 = bf16[32,256,256]{2,0,1:T(8,128)(2,1)} fusion(bf16[256,50,256]{2,0,1:T(8,128)(2,1)} %param.17, f32[32,50]{1,0:T(8,128)S(1)} %convolution_add_fusion.1), kind=kOutput, calls=%fused_computation.12 | convolution fusion | flops 211820352 | bytes 10754304 | tf_op jit(solution)/shard_map/kh,dhc->kdc/dot_general | solution.py:73
  51.6 19.6 %all-to-all-done = bf16[16,2,16384]{2,1,0:T(2,128)(2,1)S(1)} async-done(((bf16[16,2,16384]{2,1,0:T(2,128)(2,1)}), bf16[16,2,16384]{2,1,0:T(2,128)(2,1)S(1)}, u32[]{:S(2)}, u32[]{:S(2)}) %all-to-all-start) | async-done | bytes 1048608 | tf_op jit(solution)/shard_map/all_to_all | solution.py:76
  71.2 1.3 reshape.51
  72.5 1.2 copy.36
  73.8 5.9 fusion.7
  79.7 0.0 reduce-scatter.4.cloned.1.call-update
  79.7 0.2 all-gather.2.cloned.1.call-start
  80.0 81.4 %reduce-scatter.4.cloned.1.call-done = f32[2,64,256]{2,1,0:T(8,128)} async-done(((f32[32,64,256]{2,1,0:T(8,128)}), f32[2,64,256]{2,1,0:T(8,128)}) %reduce-scatter.4.cloned.1.call-update) | async-done | bytes 131088 | tf_op jit(solution)/shard_map/reduce_scatter | solution.py:77
  161.4 0.0 copy-done.9
  161.4 1.9 fusion.20
  163.3 0.0 all-gather.2.cloned.1.call-update
  163.3 53.8 %all-gather.2.cloned.1.call-done = bf16[32,64,256]{2,1,0:T(8,128)(2,1)} async-done(((bf16[2,64,256]{2,1,0:T(8,128)(2,1)}), bf16[32,64,256]{2,1,0:T(8,128)(2,1)}) %all-gather.2.cloned.1.call-update) | async-done | bytes 1048592 | tf_op jit(solution)/shard_map/all_gather | solution.py:84
  217.1 6.0 fusion.12
  223.1 4.3 all-to-all-start.2
  227.4 0.0 copy-start.2
  227.4 0.0 all-reduce.7.cloned.1.call-start
  227.4 11.4 %copy.42 = bf16[256,50,256]{0,1,2:T(8,128)(2,1)} copy(bf16[256,50,256]{2,0,1:T(8,128)(2,1)} %param.17) | data formatting | bytes 13107200 | tf_op args[8]
  238.8 3.4 convolution_convert_fusion
  242.2 7.9 copy.41
  250.1 6.4 fusion.30
  256.5 1.0 fusion.21
  257.6 1.4 all-to-all-done.2
  258.9 0.6 copy.40
  259.6 0.0 copy-start.3
  259.6 1.7 copy.46
  261.2 0.0 copy-start.6
  261.3 0.8 convert_reduce_fusion
  262.1 0.0 copy-done.6
  262.1 1.8 convolution_bitcast_fusion
  263.9 0.0 all-reduce.7.cloned.1.call-update
  263.9 0.3 reduce-scatter.6.cloned.1.call-start
  264.2 8.2 convert_bitcast_fusion
  272.4 0.0 reduce-scatter.6.cloned.1.call-update
  272.4 0.0 all-reduce.9.cloned.1.call-start
  272.5 181.0 %all-reduce.7.cloned.1.call-done = (f32[128,4096]{0,1:T(8,128)}, f32[512,128]{1,0:T(8,128)}) async-done(((f32[128,4096]{0,1:T(8,128)}, f32[512,128]{1,0:T(8,128)}), (f32[128,4096]{0,1:T(8,128)}, f32[512,128]{1,0:T(8,128)})) %all-reduce.7.cloned.1.call-update) | async-done | bytes 2359312 | tf_op jit(solution)/shard_map/psum | solution.py:16
  453.5 0.0 all-reduce.9.cloned.1.call-update
  453.5 0.0 reduce-scatter.8.cloned.1.call-start
  453.6 78.6 %reduce-scatter.6.cloned.1.call-done = bf16[64,50,256]{2,1,0:T(8,128)(2,1)} async-done(((bf16[256,50,256]{2,1,0:T(8,128)(2,1)}), bf16[64,50,256]{2,1,0:T(8,128)(2,1)}) %reduce-scatter.6.cloned.1.call-update) | async-done | bytes 1638416 | tf_op jit(solution)/shard_map/reduce_scatter | solution.py:39
  532.1 0.0 reduce-scatter.8.cloned.1.call-update
  532.1 0.2 fusion.31
  532.3 311.4 %all-reduce = (f32[4096]{0:T(1024)S(1)}, f32[128,50]{0,1:T(8,128)S(1)}, f32[50]{0:T(128)S(1)}) all-reduce(f32[4096]{0:T(1024)S(1)} %get-tuple-element.34, f32[128,50]{0,1:T(8,128)S(1)} %fusion.31, f32[50]{0:T(128)S(1)} %get-tuple-element.38), channel_id=1, replica_groups=mesh['dp_0'=4,'dp_1'=4,'hyper'=16] {'dp_1','hyper'}, use_global_device_ids=true, to_apply=%region_6.7 | all-reduce | flops 10546 | bytes 84368 | tf_op jit(solution)/shard_map/psum | solution.py:16
  843.7 17.1 %all-reduce.2 = (f32[4096]{0:T(1024)}, f32[128,50]{0,1:T(8,128)}, f32[50]{0:T(128)}) all-reduce(f32[4096]{0:T(1024)S(1)} %get-tuple-element.24, f32[128,50]{0,1:T(8,128)S(1)} %get-tuple-element.25, f32[50]{0:T(128)S(1)} %get-tuple-element.26), channel_id=1, replica_groups=mesh['dp_0'=4,'dp_1'=4,'hyper'=16] {'dp_0'}, use_global_device_ids=true, to_apply=%region_7.8 | all-reduce | flops 10546 | bytes 84368 | tf_op jit(solution)/shard_map/psum | solution.py:16
  860.9 3.0 copy.44
  863.9 2.0 copy.45
  865.9 0.7 copy.63
  (12 shorter events, 0.0 us)
Async XLA Ops:
  7.2 12.4 %copy-start = (bf16[128,4096]{1,0:T(8,128)(2,1)S(1)}, bf16[128,4096]{1,0:T(8,128)(2,1)}, u32[]{:S(2)}) copy-start(bf16[128,4096]{1,0:T(8,128)(2,1)} %param.12) | copy-start | bytes 3145732
  8.5 21.4 %all-to-all-start.1 = ((s32[16,1,2]{2,1,0:T(1,128)}), s32[16,1,2]{2,1,0:T(1,128)S(1)}, u32[]{:S(2)}, u32[]{:S(2)}) async-start(s32[16,1,2]{2,1,0:T(1,128)} %broadcast_in_dim.2), calls=%async_computation.1 | async-start | bytes 16384 | tf_op jit(solution)/shard_map/all_to_all | solution.py:22
  27.7 13.2 %copy-start.8 = (bf16[512,128]{1,0:T(8,128)(2,1)S(1)}, bf16[512,128]{1,0:T(8,128)(2,1)}, u32[]{:S(2)}) copy-start(bf16[512,128]{1,0:T(8,128)(2,1)} %param.14) | copy-start | bytes 393220
  27.7 13.4 %copy-start.5 = (bf16[128,50]{0,1:T(8,128)(2,1)S(1)}, bf16[128,50]{0,1:T(8,128)(2,1)}, u32[]{:S(2)}) copy-start(bf16[128,50]{0,1:T(8,128)(2,1)} %param.15) | copy-start | bytes 38404
  27.7 13.4 %copy-start.7 = (f32[50]{0:T(128)S(1)}, f32[50]{0:T(128)}, u32[]{:S(2)}) copy-start(f32[50]{0:T(128)} %param.16) | copy-start | bytes 604
  30.0 41.2 %all-to-all-start = ((bf16[16,2,16384]{2,1,0:T(2,128)(2,1)}), bf16[16,2,16384]{2,1,0:T(2,128)(2,1)S(1)}, u32[]{:S(2)}, u32[]{:S(2)}) async-start(bf16[16,2,16384]{2,1,0:T(2,128)(2,1)} %reshape.50), calls=%async_computation | async-start | bytes 2097152 | tf_op jit(solution)/shard_map/all_to_all | solution.py:76
  39.6 121.8 %reduce-scatter.4.cloned.1.call-start = ((), (), s32[]{:S(2)}) async-start(), calls=%async_computation.6 | async-start | bytes 2228224 | tf_op jit(solution)/shard_map/reduce_scatter | solution.py:77
  79.7 81.7 %copy-start.9 = (s32[2,64]{1,0:T(2,128)S(1)}, s32[2,64]{1,0:T(2,128)}, u32[]{:S(2)}) copy-start(s32[2,64]{1,0:T(2,128)} %param.10) | copy-start | bytes 1540
  79.7 137.4 %all-gather.2.cloned.1.call-start = ((), (), s32[]{:S(2)}) async-start(), calls=%async_computation.7 | async-start | bytes 1114112 | tf_op jit(solution)/shard_map/all_gather | solution.py:84
  223.1 35.8 %all-to-all-start.2 = ((bf16[32,64,256]{2,1,0:T(8,128)(2,1)}), bf16[32,64,256]{2,1,0:T(8,128)(2,1)S(1)}, u32[]{:S(2)}, u32[]{:S(2)}) async-start(bf16[32,64,256]{2,1,0:T(8,128)(2,1)} %fusion.12), calls=%async_computation.3 | async-start | bytes 2097152 | tf_op jit(solution)/shard_map/all_to_all | solution.py:91
  227.4 11.4 %copy-start.2 = (bf16[32,64,256]{2,1,0:T(8,128)(2,1)S(1)}, bf16[32,64,256]{2,1,0:T(8,128)(2,1)}, u32[]{:S(2)}) copy-start(bf16[32,64,256]{2,1,0:T(8,128)(2,1)} %all-gather.2.cloned.1.call-done) | copy-start | bytes 3145732
  227.4 226.1 %all-reduce.7.cloned.1.call-start = ((), (), s32[]{:S(2)}) async-start(), calls=%async_computation.10 | async-start | bytes 4718592 | tf_op jit(solution)/shard_map/psum | solution.py:16
  259.6 1.7 copy-start.3
  261.2 0.8 copy-start.6
  263.9 268.2 %reduce-scatter.6.cloned.1.call-start = ((), (), s32[]{:S(2)}) async-start(), calls=%async_computation.8 | async-start | bytes 9175040 | tf_op jit(solution)/shard_map/reduce_scatter | solution.py:39
  272.4 588.5 %all-reduce.9.cloned.1.call-start = ((), (), s32[]{:S(2)}) async-start(), calls=%async_computation.11 | async-start | bytes 4718592 | tf_op jit(solution)/shard_map/psum | solution.py:16
  453.5 410.4 %reduce-scatter.8.cloned.1.call-start = ((), (), s32[]{:S(2)}) async-start(), calls=%async_computation.9 | async-start | bytes 2293760 | tf_op jit(solution)/shard_map/reduce_scatter | solution.py:39
  860.9 5.7 copy-start.1
  860.9 5.0 copy-start.4
Sparse Core Ops, SparseCore 0:
  79.9 81.5 reduce-scatter.3
  164.7 52.3 all-gather.1
  264.0 189.3 all-reduce.6
  455.9 76.1 reduce-scatter.5
  534.4 67.7 all-reduce.8
  604.6 44.2 reduce-scatter.7
